TPU v7x, 32 devices: a whole 2x2x4 slice. The times are simulated.
32 devices in a mesh: gx: 4 (over y, x), gy: 4 (over z), gz: 2 (over core).
Axes of the slice: x: 2, y: 2, z: 4, core: 2. Of those that a mesh axis runs over, the one named last changes fastest.
Arguments:
- density: float32 [32, 256, 256], P('gx', 'gy', 'gz'), may hold values from 0.2 to 6, as said below
- momentum: float32 [3, 32, 256, 256], P(None, 'gx', 'gy', 'gz'), may hold values from -6 to 6
- energy: float32 [32, 256, 256], P('gx', 'gy', 'gz'), may hold values from 0.2 to 6, as said below
- displacement: int32 [3, 32, 256, 256], P(None, 'gx', 'gy', 'gz'), may hold values from -255 to 255
- flags: int32 [6], replicated, may hold values from 0 to 1
Outputs:
- new_density: float32 [32, 256, 256], P('gx', 'gy', 'gz')
- new_momentum: float32 [3, 32, 256, 256], P(None, 'gx', 'gy', 'gz')
- new_energy: float32 [32, 256, 256], P('gx', 'gy', 'gz')
- totals: float32 [2], replicated
Inputs may be any that keep to these rules, and one draw needn't show every extreme that they name: density is positive. energy is positive.
All inputs are finite; a program needn't handle non-finite values.
Results may differ from a plain program's by a relative error of at most 0.0003.
Values sent between devices are 32-bit elements; how exact they have to be, the bound alone decides.
A program may use at most 64 MiB of HBM per device.

v0:
```python
import jax
import jax.numpy as jnp
from jax import lax
from jax.sharding import PartitionSpec as P


def from_behind(value, axis, steps):
    count = lax.axis_size(axis)
    leading, last = (max(0, -steps), min(count, count - steps))
    return lax.ppermute(value, axis, [(source, source + steps) for source in range(leading, last)])


def padded_2(block, sides, width):
    for axis, dim in sides:
        count = lax.axis_size(axis)
        forward = [(i, i + 1) for i in range(count - 1)]
        backward = [(target, source) for source, target in forward]
        low = lax.ppermute(
            lax.slice_in_dim(block, block.shape[dim] - width, None, axis=dim), axis, forward
        )
        high = lax.ppermute(lax.slice_in_dim(block, 0, width, axis=dim), axis, backward)
        block = jnp.concatenate([low, block, high], axis=dim)
    return block


def minmod(left_diff, right_diff):
    return (
        0.5
        * (jnp.sign(left_diff) + jnp.sign(right_diff))
        * jnp.minimum(jnp.abs(left_diff), jnp.abs(right_diff))
    )


def flux_change(padded, face_rows, along):
    total_len = padded.shape[along]
    upper_cells = lax.slice_in_dim(padded, 2, total_len, axis=along)
    middle = lax.slice_in_dim(padded, 1, total_len - 1, axis=along)
    lower_cells = lax.slice_in_dim(padded, 0, total_len - 2, axis=along)
    slopes = minmod(upper_cells - middle, middle - lower_cells)
    k = total_len - 2
    low_val = lax.slice_in_dim(middle, 0, k - 1, axis=along)
    high_val = lax.slice_in_dim(middle, 1, k, axis=along)
    low_slope = lax.slice_in_dim(slopes, 0, k - 1, axis=along)
    high_slope = lax.slice_in_dim(slopes, 1, k, axis=along)
    fluxes = face_rows * jnp.where(
        face_rows > 0,
        low_val + 0.5 * (1.0 - face_rows) * low_slope,
        high_val - 0.5 * (1.0 + face_rows) * high_slope,
    )
    m = k - 1
    return lax.slice_in_dim(fluxes, 0, m - 1, axis=along) - lax.slice_in_dim(
        fluxes, 1, m, axis=along
    )


def fix_ghosts(padded, along, position, count_on):
    total_len = padded.shape[along]
    first_cell = lax.slice_in_dim(padded, 2, 3, axis=along)
    last_cell = lax.slice_in_dim(padded, total_len - 3, total_len - 2, axis=along)
    low_ghosts = jnp.where(
        position == 0,
        jnp.concatenate([first_cell, first_cell], along),
        lax.slice_in_dim(padded, 0, 2, axis=along),
    )
    high_ghosts = jnp.where(
        position == count_on - 1,
        jnp.concatenate([last_cell, last_cell], along),
        lax.slice_in_dim(padded, total_len - 2, total_len, axis=along),
    )
    return jnp.concatenate(
        [low_ghosts, lax.slice_in_dim(padded, 2, total_len - 2, axis=along), high_ghosts], along
    )


def face_edges(face_speed, comp, position, flag_open):
    n = face_speed.shape[comp]
    low_face = lax.slice_in_dim(face_speed, 0, 1, axis=comp) * jnp.where(
        position == 0, flag_open[2 * comp], 1.0
    )
    last_face = lax.slice_in_dim(face_speed, n - 1, n, axis=comp) * flag_open[2 * comp + 1]
    return (low_face, last_face)


def face_build(face_speed, comp, next_plane, position, count_on, flag_open):
    n = face_speed.shape[comp]
    low_face, last_face = face_edges(face_speed, comp, position, flag_open)
    high_face = jnp.where(
        position == count_on - 1, last_face, next_plane.astype(jnp.float32) / 256.0
    )
    face_rows = jnp.concatenate(
        [low_face, lax.slice_in_dim(face_speed, 1, n, axis=comp), high_face], comp
    )
    return face_rows[None]


def shards(density, momentum, energy, displacement, flags):
    fields = jnp.concatenate([density[None], momentum, energy[None]], 0)
    face_speed = displacement.astype(jnp.float32) / 256.0
    flag_open = flags.astype(jnp.float32)
    pos_x, pos_y, pos_z = (lax.axis_index("gx"), lax.axis_index("gy"), lax.axis_index("gz"))
    size_x, size_y, size_z = (lax.axis_size("gx"), lax.axis_size("gy"), lax.axis_size("gz"))
    cell_total = float(
        fields.shape[1] * fields.shape[2] * fields.shape[3] * size_x * size_y * size_z
    )
    next_xplane = from_behind(displacement[0, 0:1], "gx", -1)
    next_yplane = from_behind(displacement[1, :, 0:1], "gy", -1)
    next_zplane = from_behind(displacement[2, :, :, 0:1], "gz", -1)
    faces_x = face_build(face_speed[0], 0, next_xplane, pos_x, size_x, flag_open)
    faces_y = face_build(face_speed[1], 1, next_yplane, pos_y, size_y, flag_open)
    faces_z = face_build(face_speed[2], 2, next_zplane, pos_z, size_z, flag_open)
    along_x = padded_2(fields, (("gx", 1),), 2)
    along_y = padded_2(fields, (("gy", 2),), 2)
    along_z = padded_2(fields, (("gz", 3),), 2)
    updated = fields + flux_change(fix_ghosts(along_x, 1, pos_x, size_x), faces_x, 1)
    updated = updated + flux_change(fix_ghosts(along_y, 2, pos_y, size_y), faces_y, 2)
    updated = updated + flux_change(fix_ghosts(along_z, 3, pos_z, size_z), faces_z, 3)
    mass_sum, energy_sum = lax.psum((jnp.sum(updated[0]), jnp.sum(updated[4])), ("gx", "gy", "gz"))
    totals = jnp.stack([mass_sum, energy_sum]) / cell_total
    return (updated[0], updated[1:4], updated[4], totals)


def solution(mesh):
    return jax.shard_map(
        shards,
        mesh=mesh,
        in_specs=(
            P("gx", "gy", "gz"),
            P(None, "gx", "gy", "gz"),
            P("gx", "gy", "gz"),
            P(None, "gx", "gy", "gz"),
            P(),
        ),
        out_specs=(P("gx", "gy", "gz"), P(None, "gx", "gy", "gz"), P("gx", "gy", "gz"), P()),
        check_vma=False,
    )
```

profile of v0, /device:TPU:0, one launch (start us, length us, event | category | flops | bytes accessed | tf_op | source)
XLA Modules:
  0.0 120.2 jit_solution(10751196906076878649)
XLA Ops:
  0.6 1.4 %pad_maximum_fusion.15 = f32[5,8,64,128]{3,2,1,0:T(8,128)S(1)} fusion(f32[1,8,64,128]{3,2,1,0:T(8,128)} %bitcast.35, f32[3,8,64,128]{3,2,1,0:T(8,128)} %param.6, f32[1,8,64,128]{3,2,1,0:T(8,128)} %bitcast.43), kind=kLoop, calls=%fused_computation.45 | loop fusion | flops 655360 | bytes 2621440 | tf_op jit(solution)/shard_map/concatenate | solution.py:97
  2.0 1.6 %fusion.24 = (f32[5,8,64,2]{3,2,1,0:T(8,128)}, f32[5,8,64,2]{3,2,1,0:T(8,128)S(1)}) fusion(f32[5,8,64,128]{3,2,1,0:T(8,128)S(1)} %pad_maximum_fusion.15), kind=kLoop, calls=%fused_computation.91 | loop fusion | bytes 81920 | tf_op jit(solution)/shard_map/slice | solution.py:19
  3.5 2.4 %copy.143 = f32[5,8,64,2]{2,1,3,0:T(8,128)} copy(f32[5,8,64,2]{3,2,1,0:T(8,128)} %get-tuple-element.32) | data formatting | bytes 40960 | tf_op jit(solution)/shard_map/slice | solution.py:19
  6.0 3.0 %collective-permute-start.7 = (f32[5,8,64,2]{2,1,3,0:T(8,128)}, f32[5,8,64,2]{2,1,3,0:T(8,128)}, u32[]{:S(2)}, u32[]{:S(2)}) collective-permute-start(f32[5,8,64,2]{2,1,3,0:T(8,128)} %copy.143), channel_id=1, source_target_pairs={{0,1},{2,3},{4,5},{6,7},{8,9},{10,11},{12,13},{14,15},{16,17},{18,... | collective-permute-start | bytes 61448 | tf_op jit(solution)/shard_map/ppermute | solution.py:18
  9.0 1.1 copy.145
  10.0 1.3 %collective-permute-start.8 = (f32[5,8,64,2]{2,1,3,0:T(8,128)}, f32[5,8,64,2]{2,1,3,0:T(8,128)}, u32[]{:S(2)}, u32[]{:S(2)}) collective-permute-start(f32[5,8,64,2]{2,1,3,0:T(8,128)} %copy.145), channel_id=1, source_target_pairs={{1,0},{3,2},{5,4},{7,6},{9,8},{11,10},{13,12},{15,14},{17,16},{19,... | collective-permute-start | bytes 61448 | tf_op jit(solution)/shard_map/ppermute | solution.py:21
  11.4 0.1 copy.148
  11.5 0.9 copy.142
  12.4 1.3 %collective-permute-start.6 = (s32[8,64,1]{2,1,0:T(8,128)}, s32[8,64,1]{2,1,0:T(8,128)}, u32[]{:S(2)}, u32[]{:S(2)}) collective-permute-start(s32[8,64,1]{2,1,0:T(8,128)} %copy.142), channel_id=1, source_target_pairs={{1,0},{3,2},{5,4},{7,6},{9,8},{11,10},{13,12},{15,14},{17,16},{19,... | collective-permute-start | bytes 6152 | tf_op jit(solution)/shard_map/ppermute | solution.py:10
  13.7 0.6 copy.137
  14.3 4.9 %collective-permute-start.4 = (f32[5,8,2,128]{3,1,2,0:T(8,128)}, f32[5,8,2,128]{3,1,2,0:T(8,128)}, u32[]{:S(2)}, u32[]{:S(2)}) collective-permute-start(f32[5,8,2,128]{3,1,2,0:T(8,128)} %copy.137), channel_id=1, source_target_pairs={{0,2},{2,4},{4,6},{1,3},{3,5},{5,7},{8,10},{10,12},{12,14},{9,11},... | collective-permute-start | bytes 122888 | tf_op jit(solution)/shard_map/ppermute | solution.py:18
  19.2 0.6 copy.139
  19.8 1.3 %collective-permute-start.5 = (f32[5,8,2,128]{3,1,2,0:T(8,128)}, f32[5,8,2,128]{3,1,2,0:T(8,128)}, u32[]{:S(2)}, u32[]{:S(2)}) collective-permute-start(f32[5,8,2,128]{3,1,2,0:T(8,128)} %copy.139), channel_id=1, source_target_pairs={{2,0},{4,2},{6,4},{3,1},{5,3},{7,5},{10,8},{12,10},{14,12},{11,9},... | collective-permute-start | bytes 122888 | tf_op jit(solution)/shard_map/ppermute | solution.py:21
  21.1 2.0 %fusion.23 = (f32[5,8,64,1]{3,2,1,0:T(8,128)}, f32[5,8,64,1]{3,2,1,0:T(8,128)}) fusion(f32[5,8,64,128]{3,2,1,0:T(8,128)S(1)} %pad_maximum_fusion.15), kind=kLoop, calls=%fused_computation.90 | loop fusion | bytes 40960 | tf_op jit(solution)/shard_map/slice | solution.py:58
  23.1 0.1 convert_multiply_fusion
  23.2 0.0 copy-start.4
  23.2 0.7 fusion.22
  23.9 0.9 fusion.20
  24.8 0.8 fusion.19
  25.6 0.6 slice_bitcast_fusion.5
  26.3 0.7 fusion.25
  27.6 0.8 slice_bitcast_fusion.6
  28.4 0.1 slice.289
  29.9 1.3 %collective-permute-start.3 = (s32[8,1,128]{2,1,0:T(1,128)S(1)}, s32[8,1,128]{2,1,0:T(1,128)S(1)}, u32[]{:S(2)}, u32[]{:S(2)}) collective-permute-start(s32[8,1,128]{2,1,0:T(1,128)S(1)} %slice_bitcast_fusion.6), channel_id=1, source_target_pairs={{2,0},{4,2},{6,4},{3,1},{5,3},{7,5},{10,8},{12,10},{14,12},{11,9},... | collective-permute-start | bytes 12296 | tf_op jit(solution)/shard_map/ppermute | solution.py:10
  31.2 1.8 %slice_multiply_fusion.7 = (f32[8,64,1]{2,1,0:T(8,128)S(1)}, f32[8,64,1]{2,1,0:T(8,128)S(1)}) fusion(f32[8,64,128]{2,1,0:T(8,128)S(1)} %get-tuple-element.35, f32[]{:T(128)S(6)} %select_n.104, s32[8,64,1]{2,1,0:T(8,128)} %collective-permute-done.6, f32[]{:T(128)} %bitcast.15, pred[]{:T(512)S(6)} %eq.29), kind=kLoop, calls=%fused_computation.62 | loop fusion | flops 2560 | bytes 10249 | tf_op jit(solution)/shard_map/mul | solution.py:77
  33.0 0.2 broadcast_compare_fusion
  33.2 1.1 subtract_multiply_fusion
  34.4 1.7 %collective-permute-done.3 = s32[8,1,128]{2,1,0:T(1,128)S(1)} collective-permute-done((s32[8,1,128]{2,1,0:T(1,128)S(1)}, s32[8,1,128]{2,1,0:T(1,128)S(1)}, u32[]{:S(2)}, u32[]{:S(2)}) %collective-permute-start.3) | collective-permute-done | bytes 4128 | tf_op jit(solution)/shard_map/ppermute | solution.py:10
  36.1 4.1 %collective-permute-start.1 = (f32[5,2,64,128]{3,2,1,0:T(8,128)}, f32[5,2,64,128]{3,2,1,0:T(8,128)}, u32[]{:S(2)}, u32[]{:S(2)}) collective-permute-start(f32[5,2,64,128]{3,2,1,0:T(8,128)} %get-tuple-element.24), channel_id=1, source_target_pairs={{0,8},{8,16},{16,24},{1,9},{9,17},{17,25},{2,10},{10,18},{18,26},{... | collective-permute-start | bytes 983048 | tf_op jit(solution)/shard_map/ppermute | solution.py:18
  40.2 0.6 slice_multiply_fusion.11
  40.7 1.0 pad_maximum_fusion.18
  41.8 0.7 broadcast_compare_fusion.1
  42.5 1.3 %collective-permute-start.2 = (f32[5,2,64,128]{3,2,1,0:T(8,128)}, f32[5,2,64,128]{3,2,1,0:T(8,128)}, u32[]{:S(2)}, u32[]{:S(2)}) collective-permute-start(f32[5,2,64,128]{3,2,1,0:T(8,128)} %get-tuple-element.25), channel_id=1, source_target_pairs={{8,0},{16,8},{24,16},{9,1},{17,9},{25,17},{10,2},{18,10},{26,18},{... | collective-permute-start | bytes 983048 | tf_op jit(solution)/shard_map/ppermute | solution.py:21
  43.8 2.3 %copy.146 = f32[5,8,64,2]{3,2,1,0:T(8,128)} copy(f32[5,8,64,2]{2,1,3,0:T(8,128)} %collective-permute-done.8) | data formatting | bytes 40960 | tf_op jit(solution)/shard_map/ppermute | solution.py:21
  46.1 2.6 %maximum_select_fusion.1 = f32[5,8,64,2]{3,2,1,0:T(8,128)S(1)} fusion(f32[5,8,64,2]{3,2,1,0:T(8,128)} %copy.146, f32[5,8,64,1]{3,2,1,0:T(8,128)} %get-tuple-element.31, pred[]{:T(512)S(6)} %eq.29), kind=kLoop, calls=%fused_computation.47 | loop fusion | flops 10240 | bytes 51201 | tf_op jit(solution)/shard_map/jit(_where)/select_n | solution.py:65
  48.8 1.7 %pad_maximum_fusion.4 = f32[5,8,64,130]{3,2,1,0:T(8,128)} fusion(f32[5,8,64,2]{3,2,1,0:T(8,128)S(1)} %maximum_select_fusion.1, f32[1,8,64,128]{3,2,1,0:T(8,128)S(1)} %bitcast.36, f32[3,8,64,128]{3,2,1,0:T(8,128)S(1)} %copy-done, f32[1,8,64,128]{3,2,1,0:T(8,128)S(1)} %bitcast.44), kind=kLoop, calls=%fused_computation.11 | loop fusion | flops 998400 | bytes 2662400 | tf_op jit(solution)/shard_map/concatenate | solution.py:70
  50.5 0.0 collective-permute-done.7
  50.5 1.5 %collective-permute-start = (s32[1,64,128]{2,1,0:T(8,128)}, s32[1,64,128]{2,1,0:T(8,128)}, u32[]{:S(2)}, u32[]{:S(2)}) collective-permute-start(s32[1,64,128]{2,1,0:T(8,128)} %slice_bitcast_fusion.5), channel_id=1, source_target_pairs={{8,0},{16,8},{24,16},{9,1},{17,9},{25,17},{10,2},{18,10},{26,18},{... | collective-permute-start | bytes 98312 | tf_op jit(solution)/shard_map/ppermute | solution.py:10
  52.0 2.4 %copy.144 = f32[5,8,64,2]{3,2,1,0:T(8,128)} copy(f32[5,8,64,2]{2,1,3,0:T(8,128)} %collective-permute-done.7) | data formatting | bytes 40960 | tf_op jit(solution)/shard_map/ppermute | solution.py:18
  54.3 2.1 %maximum_select_fusion = f32[5,8,64,2]{3,2,1,0:T(8,128)S(1)} fusion(f32[5,8,64,2]{3,2,1,0:T(8,128)} %copy.144, f32[5,8,64,1]{3,2,1,0:T(8,128)} %get-tuple-element.30, pred[]{:T(512)S(6)} %eq.28), kind=kLoop, calls=%fused_computation.46 | loop fusion | flops 10240 | bytes 51201 | tf_op jit(solution)/shard_map/jit(_where)/select_n | solution.py:60
  56.5 3.1 %maximum_maximum_fusion = (f32[5,8,64,130]{3,2,1,0:T(8,128)S(1)}, f32[5,8,64,130]{3,2,1,0:T(8,128)S(1)}) fusion(f32[1,8,64,128]{3,2,1,0:T(8,128)S(1)} %bitcast.37, f32[3,8,64,128]{3,2,1,0:T(8,128)S(1)} %copy-done, f32[1,8,64,128]{3,2,1,0:T(8,128)S(1)} %bitcast.45, f32[5,8,64,2]{3,2,1,0:T(8,128)S(1)} %maximum_select_fusion, ...), kind=kLoop, calls=%fused_computation.10 | loop fusion | flops 6656000 | bytes 4014080 | tf_op jit(solution)/shard_map/concatenate | solution.py:70
  59.6 1.4 %fusion.2 = f32[5,8,64,129]{3,2,1,0:T(8,128)S(1)} fusion(f32[5,8,64,130]{3,2,1,0:T(8,128)S(1)} %get-tuple-element.15, f32[5,8,64,130]{3,2,1,0:T(8,128)S(1)} %copy-done.3, f32[5,8,64,130]{3,2,1,0:T(8,128)S(1)} %get-tuple-element.14, f32[8,64,129]{2,1,0:T(8,128)S(1)} %copy-done.6, f32[8,64,129]{2,1,0:T(8,128)S(1)} %copy-done.5, ...), kind=kLoop, calls=%fused_computation.3 | loop fusion | flops 1981440 | bytes 7463424 | tf_op jit(solution)/shard_map/mul | solution.py:45
  61.1 1.5 %fusion.17 = f32[1,64,128]{2,1,0:T(8,128)S(1)} fusion(f32[3,8,64,128]{3,2,1,0:T(8,128)} %copy-done.4, s32[1,64,128]{2,1,0:T(8,128)} %collective-permute-done, f32[]{:T(128)} %bitcast.5, pred[]{:T(512)S(6)} %eq.25), kind=kLoop, calls=%fused_computation.77 | loop fusion | flops 32768 | bytes 98309 | tf_op jit(solution)/shard_map/jit(_where)/select_n | solution.py:87
  62.5 0.1 pad_maximum_fusion.17
  62.7 0.0 collective-permute-done.5
  62.7 0.8 maximum_select_fusion.5
  63.5 0.1 pad_maximum_fusion.14
  63.7 0.0 collective-permute-done.4
  63.7 0.8 maximum_select_fusion.4
  64.5 0.0 copy-start.13
  64.6 1.3 %maximum_maximum_fusion.2 = (f32[5,8,66,128]{3,2,1,0:T(8,128)S(1)}, f32[5,8,66,128]{3,2,1,0:T(8,128)S(1)}) fusion(f32[1,8,64,128]{3,2,1,0:T(8,128)S(1)} %bitcast.39, f32[3,8,64,128]{3,2,1,0:T(8,128)S(1)} %copy-done, f32[1,8,64,128]{3,2,1,0:T(8,128)S(1)} %bitcast.47, f32[5,8,2,128]{3,2,1,0:T(2,128)S(1)} %maximum_select_fusion.4, ...), kind=kLoop, calls=%fused_computation.36 | loop fusion | flops 6758400 | bytes 4096000 | tf_op jit(solution)/shard_map/concatenate | solution.py:70
  65.9 0.5 fusion.6
  66.4 0.4 copy-done.12
  66.8 1.0 maximum_select_fusion.3
  67.8 0.0 copy-start.11
  67.8 0.1 pad_maximum_fusion.9
  68.0 0.8 copy-done.11
  68.8 1.2 %maximum_maximum_fusion.1 = (f32[5,10,64,128]{3,2,1,0:T(8,128)S(1)}, f32[5,10,64,128]{3,2,1,0:T(8,128)S(1)}) fusion(f32[1,8,64,128]{3,2,1,0:T(8,128)S(1)} %bitcast.41, f32[3,8,64,128]{3,2,1,0:T(8,128)S(1)} %copy-done, f32[1,8,64,128]{3,2,1,0:T(8,128)S(1)} %bitcast.49, f32[5,2,64,128]{3,2,1,0:T(8,128)S(1)} %maximum_select_fusion.2, ...), kind=kLoop, calls=%fused_computation.17 | loop fusion | flops 8192000 | bytes 5242880 | tf_op jit(solution)/shard_map/concatenate | solution.py:70
  70.0 0.6 fusion.10
  70.7 0.8 fusion.12
  71.4 1.5 %slice_reduce_fusion.1 = (f32[]{:T(128)}, f32[]{:T(128)}, f32[8,64,128]{2,1,0:T(8,128)}, f32[8,64,128]{2,1,0:T(8,128)}) fusion(f32[5,8,64,128]{3,2,1,0:T(8,128)S(1)} %fusion.12), kind=kLoop, calls=%fused_computation.68 | loop fusion | flops 131070 | bytes 1048584 | tf_op jit(solution)/shard_map/reduce_sum | solution.py:117
  72.9 0.9 slice.302
  73.9 44.5 %all-reduce = (f32[1]{0:T(128)}, f32[1]{0:T(128)}) all-reduce(f32[1]{0:T(128)} %bitcast.20, f32[1]{0:T(128)} %bitcast.19), channel_id=1, replica_groups=mesh['gx'=4,'gy'=4,'gz'=2] {'gx','gy','gz'}, use_global_device_ids=true, to_apply=%region_3.4 | all-reduce | flops 2 | bytes 16 | tf_op jit(solution)/shard_map/psum | solution.py:117
  118.4 1.8 %maximum_multiply_fusion = f32[2]{0:T(128)} fusion(f32[1]{0:T(128)} %get-tuple-element.10, f32[1]{0:T(128)} %get-tuple-element.11), kind=kLoop, calls=%fused_computation.85 | loop fusion | flops 4 | bytes 16 | tf_op jit(solution)/shard_map/div | solution.py:118
  (43 shorter events, 0.3 us)
Async XLA Ops:
  3.5 7.8 %copy-start.7 = (s32[3,8,64,128]{3,2,1,0:T(8,128)S(1)}, s32[3,8,64,128]{3,2,1,0:T(8,128)}, u32[]{:S(2)}) copy-start(s32[3,8,64,128]{3,2,1,0:T(8,128)} %param.8) | copy-start | bytes 2359300
  6.0 44.5 %collective-permute-start.7 = (f32[5,8,64,2]{2,1,3,0:T(8,128)}, f32[5,8,64,2]{2,1,3,0:T(8,128)}, u32[]{:S(2)}, u32[]{:S(2)}) collective-permute-start(f32[5,8,64,2]{2,1,3,0:T(8,128)} %copy.143), channel_id=1, source_target_pairs={{0,1},{2,3},{4,5},{6,7},{8,9},{10,11},{12,13},{14,15},{16,17},{18,... | collective-permute-start | bytes 61448 | tf_op jit(solution)/shard_map/ppermute | solution.py:18
  10.0 32.5 %collective-permute-start.8 = (f32[5,8,64,2]{2,1,3,0:T(8,128)}, f32[5,8,64,2]{2,1,3,0:T(8,128)}, u32[]{:S(2)}, u32[]{:S(2)}) collective-permute-start(f32[5,8,64,2]{2,1,3,0:T(8,128)} %copy.145), channel_id=1, source_target_pairs={{1,0},{3,2},{5,4},{7,6},{9,8},{11,10},{13,12},{15,14},{17,16},{19,... | collective-permute-start | bytes 61448 | tf_op jit(solution)/shard_map/ppermute | solution.py:21
  12.4 17.6 %collective-permute-start.6 = (s32[8,64,1]{2,1,0:T(8,128)}, s32[8,64,1]{2,1,0:T(8,128)}, u32[]{:S(2)}, u32[]{:S(2)}) collective-permute-start(s32[8,64,1]{2,1,0:T(8,128)} %copy.142), channel_id=1, source_target_pairs={{1,0},{3,2},{5,4},{7,6},{9,8},{11,10},{13,12},{15,14},{17,16},{19,... | collective-permute-start | bytes 6152 | tf_op jit(solution)/shard_map/ppermute | solution.py:10
  14.3 49.3 %collective-permute-start.4 = (f32[5,8,2,128]{3,1,2,0:T(8,128)}, f32[5,8,2,128]{3,1,2,0:T(8,128)}, u32[]{:S(2)}, u32[]{:S(2)}) collective-permute-start(f32[5,8,2,128]{3,1,2,0:T(8,128)} %copy.137), channel_id=1, source_target_pairs={{0,2},{2,4},{4,6},{1,3},{3,5},{5,7},{8,10},{10,12},{12,14},{9,11},... | collective-permute-start | bytes 122888 | tf_op jit(solution)/shard_map/ppermute | solution.py:18
  19.8 42.8 %collective-permute-start.5 = (f32[5,8,2,128]{3,1,2,0:T(8,128)}, f32[5,8,2,128]{3,1,2,0:T(8,128)}, u32[]{:S(2)}, u32[]{:S(2)}) collective-permute-start(f32[5,8,2,128]{3,1,2,0:T(8,128)} %copy.139), channel_id=1, source_target_pairs={{2,0},{4,2},{6,4},{3,1},{5,3},{7,5},{10,8},{12,10},{14,12},{11,9},... | collective-permute-start | bytes 122888 | tf_op jit(solution)/shard_map/ppermute | solution.py:21
  23.2 4.4 %copy-start.4 = (f32[3,8,64,128]{3,2,1,0:T(8,128)}, f32[3,8,64,128]{3,2,1,0:T(8,128)S(1)}, u32[]{:S(2)}) copy-start(f32[3,8,64,128]{3,2,1,0:T(8,128)S(1)} %convert_multiply_fusion) | copy-start | bytes 2359300
  23.9 2.3 %copy-start.16 = (s32[6]{0:T(128)S(1)}, s32[6]{0:T(128)}, u32[]{:S(2)}) copy-start(s32[6]{0:T(128)} %param.9) | copy-start | bytes 76
  29.9 6.1 %collective-permute-start.3 = (s32[8,1,128]{2,1,0:T(1,128)S(1)}, s32[8,1,128]{2,1,0:T(1,128)S(1)}, u32[]{:S(2)}, u32[]{:S(2)}) collective-permute-start(s32[8,1,128]{2,1,0:T(1,128)S(1)} %slice_bitcast_fusion.6), channel_id=1, source_target_pairs={{2,0},{4,2},{6,4},{3,1},{5,3},{7,5},{10,8},{12,10},{14,12},{11,9},... | collective-permute-start | bytes 12296 | tf_op jit(solution)/shard_map/ppermute | solution.py:10
  36.1 31.9 %collective-permute-start.1 = (f32[5,2,64,128]{3,2,1,0:T(8,128)}, f32[5,2,64,128]{3,2,1,0:T(8,128)}, u32[]{:S(2)}, u32[]{:S(2)}) collective-permute-start(f32[5,2,64,128]{3,2,1,0:T(8,128)} %get-tuple-element.24), channel_id=1, source_target_pairs={{0,8},{8,16},{16,24},{1,9},{9,17},{17,25},{2,10},{10,18},{18,26},{... | collective-permute-start | bytes 983048 | tf_op jit(solution)/shard_map/ppermute | solution.py:18
  42.5 23.9 %collective-permute-start.2 = (f32[5,2,64,128]{3,2,1,0:T(8,128)}, f32[5,2,64,128]{3,2,1,0:T(8,128)}, u32[]{:S(2)}, u32[]{:S(2)}) collective-permute-start(f32[5,2,64,128]{3,2,1,0:T(8,128)} %get-tuple-element.25), channel_id=1, source_target_pairs={{8,0},{16,8},{24,16},{9,1},{17,9},{25,17},{10,2},{18,10},{26,18},{... | collective-permute-start | bytes 983048 | tf_op jit(solution)/shard_map/ppermute | solution.py:21
  46.1 2.6 %copy-start = (f32[3,8,64,128]{3,2,1,0:T(8,128)S(1)}, f32[3,8,64,128]{3,2,1,0:T(8,128)}, u32[]{:S(2)}) copy-start(f32[3,8,64,128]{3,2,1,0:T(8,128)} %param.6) | copy-start | bytes 2359300
  46.1 2.6 %copy-start.1 = (f32[8,64,128]{2,1,0:T(8,128)S(1)}, f32[8,64,128]{2,1,0:T(8,128)}, u32[]{:S(2)}) copy-start(f32[8,64,128]{2,1,0:T(8,128)} %param.7) | copy-start | bytes 786436
  46.1 2.6 %copy-start.2 = (f32[8,64,128]{2,1,0:T(8,128)S(1)}, f32[8,64,128]{2,1,0:T(8,128)}, u32[]{:S(2)}) copy-start(f32[8,64,128]{2,1,0:T(8,128)} %param.5) | copy-start | bytes 786436
  50.5 10.6 %collective-permute-start = (s32[1,64,128]{2,1,0:T(8,128)}, s32[1,64,128]{2,1,0:T(8,128)}, u32[]{:S(2)}, u32[]{:S(2)}) collective-permute-start(s32[1,64,128]{2,1,0:T(8,128)} %slice_bitcast_fusion.5), channel_id=1, source_target_pairs={{8,0},{16,8},{24,16},{9,1},{17,9},{25,17},{10,2},{18,10},{26,18},{... | collective-permute-start | bytes 98312 | tf_op jit(solution)/shard_map/ppermute | solution.py:10
  56.5 3.1 %copy-start.3 = (f32[5,8,64,130]{3,2,1,0:T(8,128)S(1)}, f32[5,8,64,130]{3,2,1,0:T(8,128)}, u32[]{:S(2)}) copy-start(f32[5,8,64,130]{3,2,1,0:T(8,128)} %pad_maximum_fusion.4) | copy-start | bytes 3993604
  56.5 3.1 %copy-start.5 = (f32[8,64,129]{2,1,0:T(8,128)S(1)}, f32[8,64,129]{2,1,0:T(8,128)}, u32[]{:S(2)}) copy-start(f32[8,64,129]{2,1,0:T(8,128)} %get-tuple-element.36) | copy-start | bytes 792580
  56.5 3.1 %copy-start.6 = (f32[8,64,129]{2,1,0:T(8,128)S(1)}, f32[8,64,129]{2,1,0:T(8,128)}, u32[]{:S(2)}) copy-start(f32[8,64,129]{2,1,0:T(8,128)} %get-tuple-element.37) | copy-start | bytes 792580
  61.1 1.6 %copy-start.15 = (f32[5,8,1,128]{3,2,1,0:T(1,128)S(1)}, f32[5,8,1,128]{3,2,1,0:T(1,128)}, u32[]{:S(2)}) copy-start(f32[5,8,1,128]{3,2,1,0:T(1,128)} %get-tuple-element.29) | copy-start | bytes 61444
  62.7 1.0 copy-start.14
  64.5 1.3 %copy-start.8 = (f32[8,65,128]{2,1,0:T(8,128)S(1)}, f32[8,65,128]{2,1,0:T(8,128)}, u32[]{:S(2)}) copy-start(f32[8,65,128]{2,1,0:T(8,128)} %get-tuple-element.41) | copy-start | bytes 798724
  64.5 1.3 %copy-start.9 = (f32[8,65,128]{2,1,0:T(8,128)S(1)}, f32[8,65,128]{2,1,0:T(8,128)}, u32[]{:S(2)}) copy-start(f32[8,65,128]{2,1,0:T(8,128)} %get-tuple-element.42) | copy-start | bytes 798724
  64.5 1.3 %copy-start.10 = (f32[8,65,128]{2,1,0:T(8,128)S(1)}, f32[8,65,128]{2,1,0:T(8,128)}, u32[]{:S(2)}) copy-start(f32[8,65,128]{2,1,0:T(8,128)} %get-tuple-element.43) | copy-start | bytes 798724
  64.5 1.3 %copy-start.13 = (pred[8,65,128]{2,1,0:T(8,128)(4,1)S(1)}, pred[8,65,128]{2,1,0:T(8,128)(4,1)}, u32[]{:S(2)}) copy-start(pred[8,65,128]{2,1,0:T(8,128)(4,1)} %broadcast_compare_fusion.1) | copy-start | bytes 199684
  65.9 0.9 copy-start.12
  67.8 0.9 copy-start.11
where the time goes:
time: 121 us; the launch traced here: 120 us
  blocking collectives  44.5 us (37%)
  other arithmetic  30.2 us (25%)
  local copies, waits for them, and re-layouts  20.8 us (17%)
  starting transfers between devices  19.9 us (16%)
  between operations  3.16 us (3%)
  waiting for transfers between devices  1.73 us (1%)
    psum x1, blocking collectives, shards(): lax.psum((jnp.sum(updated[0]), jnp.sum(updated[4])), ('gx', 'gy', 'gz'))  44.5 us
    ppermute x3, starting transfers between devices, padded_2(): lax.ppermute(lax.slice_in_dim(block, block.shape[dim] - width, None, axis...  12 us
    concatenate x6, other arithmetic, fix_ghosts(): jnp.concatenate([low_ghosts, lax.slice_in_dim(padded, 2, total_len - 2, a...  7.61 us
    slice x5, local copies, waits for them, and re-layouts, padded_2(): lax.slice_in_dim(block, block.shape[dim] - width, None, axis=dim)  5.54 us
    select_n x3, other arithmetic, fix_ghosts(): jnp.where(position == count_on - 1, jnp.concatenate([last_cell, last_cell...  4.44 us
    ppermute x3, starting transfers between devices, from_behind(): lax.ppermute(value, axis, [(source, source + steps) for source in range(l...  4.03 us
    ppermute x3, starting transfers between devices, padded_2(): lax.ppermute(lax.slice_in_dim(block, 0, width, axis=dim), axis, backward)  3.84 us
    slice x3, local copies, waits for them, and re-layouts, fix_ghosts(): first_cell = lax.slice_in_dim(padded, 2, 3, axis=along)  3.47 us
  transfers between devices with their start and end apart: 9, of which 1 were waited for; matrix products, arithmetic and copies ran while one was open for 31% of the time, Pallas kernels for 0%

commit v1 on v0

--- a/solution.py
+++ b/solution.py
@@ -114,7 +114,9 @@
     updated = fields + flux_change(fix_ghosts(along_x, 1, pos_x, size_x), faces_x, 1)
     updated = updated + flux_change(fix_ghosts(along_y, 2, pos_y, size_y), faces_y, 2)
     updated = updated + flux_change(fix_ghosts(along_z, 3, pos_z, size_z), faces_z, 3)
-    mass_sum, energy_sum = lax.psum((jnp.sum(updated[0]), jnp.sum(updated[4])), ("gx", "gy", "gz"))
+    mass_sum, energy_sum = lax.psum(
+        lax.psum((jnp.sum(updated[0]), jnp.sum(updated[4])), "gx"), ("gy", "gz")
+    )
     totals = jnp.stack([mass_sum, energy_sum]) / cell_total
     return (updated[0], updated[1:4], updated[4], totals)
 

time: 121 us -> 106 us (0.88)
  blocking collectives: 44.5 us -> 29.3 us
    psum x1 -> x2, blocking collectives: 44.5 us -> 29.3 us  [the longest x1 15.9 us: shards(): lax.psum(lax.psum((jnp.sum(updated[0]), jnp.sum(updated[4])), 'gx'), ('gy...]
  transfers between devices with their start and end apart: 9 -> 9, of which waited for: 1 -> 1; matrix products, arithmetic and copies ran while one was open for 31% -> 36% of each run, Pallas kernels for 0% -> 0%
where the time goes in v1:
time: 106 us; the launch traced here: 105 us
  other arithmetic  30 us (28%)
  blocking collectives  29.3 us (28%)
  local copies, waits for them, and re-layouts  20.7 us (20%)
  starting transfers between devices  19.9 us (19%)
  between operations  2.96 us (3%)
  waiting for transfers between devices  1.81 us (2%)
    psum x1, blocking collectives, shards(): lax.psum(lax.psum((jnp.sum(updated[0]), jnp.sum(updated[4])), 'gx'), ('gy...  15.9 us
    psum x1, blocking collectives, shards(): lax.psum((jnp.sum(updated[0]), jnp.sum(updated[4])), 'gx')  13.4 us
    ppermute x3, starting transfers between devices, padded_2(): lax.ppermute(lax.slice_in_dim(block, block.shape[dim] - width, None, axis...  12 us
    concatenate x6, other arithmetic, fix_ghosts(): jnp.concatenate([low_ghosts, lax.slice_in_dim(padded, 2, total_len - 2, a...  7.62 us
    slice x5, local copies, waits for them, and re-layouts, padded_2(): lax.slice_in_dim(block, block.shape[dim] - width, None, axis=dim)  5.54 us
    select_n x3, other arithmetic, fix_ghosts(): jnp.where(position == count_on - 1, jnp.concatenate([last_cell, last_cell...  4.44 us
    ppermute x3, starting transfers between devices, from_behind(): lax.ppermute(value, axis, [(source, source + steps) for source in range(l...  4.03 us
    ppermute x3, starting transfers between devices, padded_2(): lax.ppermute(lax.slice_in_dim(block, 0, width, axis=dim), axis, backward)  3.84 us
  transfers between devices with their start and end apart: 9, of which 1 were waited for; matrix products, arithmetic and copies ran while one was open for 36% of the time, Pallas kernels for 0%

profile of v1, /device:TPU:0, one launch (start us, length us, event | category | flops | bytes accessed | tf_op | source)
XLA Modules:
  0.0 104.8 jit_solution(1482250398412368108)
XLA Ops:
  0.6 1.4 %pad_maximum_fusion.15 = f32[5,8,64,128]{3,2,1,0:T(8,128)S(1)} fusion(f32[1,8,64,128]{3,2,1,0:T(8,128)} %bitcast.35, f32[3,8,64,128]{3,2,1,0:T(8,128)} %param.6, f32[1,8,64,128]{3,2,1,0:T(8,128)} %bitcast.43), kind=kLoop, calls=%fused_computation.45 | loop fusion | flops 655360 | bytes 2621440 | tf_op jit(solution)/shard_map/concatenate | solution.py:97
  2.0 1.6 %fusion.24 = (f32[5,8,64,2]{3,2,1,0:T(8,128)}, f32[5,8,64,2]{3,2,1,0:T(8,128)S(1)}) fusion(f32[5,8,64,128]{3,2,1,0:T(8,128)S(1)} %pad_maximum_fusion.15), kind=kLoop, calls=%fused_computation.91 | loop fusion | bytes 81920 | tf_op jit(solution)/shard_map/slice | solution.py:19
  3.5 2.4 %copy.143 = f32[5,8,64,2]{2,1,3,0:T(8,128)} copy(f32[5,8,64,2]{3,2,1,0:T(8,128)} %get-tuple-element.34) | data formatting | bytes 40960 | tf_op jit(solution)/shard_map/slice | solution.py:19
  6.0 3.0 %collective-permute-start.7 = (f32[5,8,64,2]{2,1,3,0:T(8,128)}, f32[5,8,64,2]{2,1,3,0:T(8,128)}, u32[]{:S(2)}, u32[]{:S(2)}) collective-permute-start(f32[5,8,64,2]{2,1,3,0:T(8,128)} %copy.143), channel_id=1, source_target_pairs={{0,1},{2,3},{4,5},{6,7},{8,9},{10,11},{12,13},{14,15},{16,17},{18,... | collective-permute-start | bytes 61448 | tf_op jit(solution)/shard_map/ppermute | solution.py:18
  9.0 1.0 copy.145
  10.0 1.3 %collective-permute-start.8 = (f32[5,8,64,2]{2,1,3,0:T(8,128)}, f32[5,8,64,2]{2,1,3,0:T(8,128)}, u32[]{:S(2)}, u32[]{:S(2)}) collective-permute-start(f32[5,8,64,2]{2,1,3,0:T(8,128)} %copy.145), channel_id=1, source_target_pairs={{1,0},{3,2},{5,4},{7,6},{9,8},{11,10},{13,12},{15,14},{17,16},{19,... | collective-permute-start | bytes 61448 | tf_op jit(solution)/shard_map/ppermute | solution.py:21
  11.4 0.1 copy.148
  11.5 0.9 copy.142
  12.4 1.3 %collective-permute-start.6 = (s32[8,64,1]{2,1,0:T(8,128)}, s32[8,64,1]{2,1,0:T(8,128)}, u32[]{:S(2)}, u32[]{:S(2)}) collective-permute-start(s32[8,64,1]{2,1,0:T(8,128)} %copy.142), channel_id=1, source_target_pairs={{1,0},{3,2},{5,4},{7,6},{9,8},{11,10},{13,12},{15,14},{17,16},{19,... | collective-permute-start | bytes 6152 | tf_op jit(solution)/shard_map/ppermute | solution.py:10
  13.7 0.6 copy.137
  14.3 4.9 %collective-permute-start.4 = (f32[5,8,2,128]{3,1,2,0:T(8,128)}, f32[5,8,2,128]{3,1,2,0:T(8,128)}, u32[]{:S(2)}, u32[]{:S(2)}) collective-permute-start(f32[5,8,2,128]{3,1,2,0:T(8,128)} %copy.137), channel_id=1, source_target_pairs={{0,2},{2,4},{4,6},{1,3},{3,5},{5,7},{8,10},{10,12},{12,14},{9,11},... | collective-permute-start | bytes 122888 | tf_op jit(solution)/shard_map/ppermute | solution.py:18
  19.2 0.6 copy.139
  19.8 1.3 %collective-permute-start.5 = (f32[5,8,2,128]{3,1,2,0:T(8,128)}, f32[5,8,2,128]{3,1,2,0:T(8,128)}, u32[]{:S(2)}, u32[]{:S(2)}) collective-permute-start(f32[5,8,2,128]{3,1,2,0:T(8,128)} %copy.139), channel_id=1, source_target_pairs={{2,0},{4,2},{6,4},{3,1},{5,3},{7,5},{10,8},{12,10},{14,12},{11,9},... | collective-permute-start | bytes 122888 | tf_op jit(solution)/shard_map/ppermute | solution.py:21
  21.1 2.0 %fusion.23 = (f32[5,8,64,1]{3,2,1,0:T(8,128)}, f32[5,8,64,1]{3,2,1,0:T(8,128)}) fusion(f32[5,8,64,128]{3,2,1,0:T(8,128)S(1)} %pad_maximum_fusion.15), kind=kLoop, calls=%fused_computation.90 | loop fusion | bytes 40960 | tf_op jit(solution)/shard_map/slice | solution.py:58
  23.1 0.1 convert_multiply_fusion
  23.2 0.0 copy-start.4
  23.2 0.7 fusion.22
  23.9 0.9 fusion.20
  24.8 0.8 fusion.19
  25.5 0.6 slice_bitcast_fusion.5
  26.2 0.6 fusion.25
  27.6 0.8 slice_bitcast_fusion.6
  28.3 0.1 slice.289
  29.7 1.3 %collective-permute-start.3 = (s32[8,1,128]{2,1,0:T(1,128)S(1)}, s32[8,1,128]{2,1,0:T(1,128)S(1)}, u32[]{:S(2)}, u32[]{:S(2)}) collective-permute-start(s32[8,1,128]{2,1,0:T(1,128)S(1)} %slice_bitcast_fusion.6), channel_id=1, source_target_pairs={{2,0},{4,2},{6,4},{3,1},{5,3},{7,5},{10,8},{12,10},{14,12},{11,9},... | collective-permute-start | bytes 12296 | tf_op jit(solution)/shard_map/ppermute | solution.py:10
  31.0 1.7 %slice_multiply_fusion.7 = (f32[8,64,1]{2,1,0:T(8,128)S(1)}, f32[8,64,1]{2,1,0:T(8,128)S(1)}) fusion(f32[8,64,128]{2,1,0:T(8,128)S(1)} %get-tuple-element.37, f32[]{:T(128)S(6)} %select_n.104, s32[8,64,1]{2,1,0:T(8,128)} %collective-permute-done.6, f32[]{:T(128)} %bitcast.15, pred[]{:T(512)S(6)} %eq.29), kind=kLoop, calls=%fused_computation.62 | loop fusion | flops 2560 | bytes 10249 | tf_op jit(solution)/shard_map/mul | solution.py:77
  32.7 0.2 broadcast_compare_fusion
  32.9 1.1 %subtract_multiply_fusion = (f32[8,64,129]{2,1,0:T(8,128)}, f32[8,64,129]{2,1,0:T(8,128)}) fusion(f32[8,64,129]{2,1,0:T(8,128)S(1)} %get-tuple-element.15), kind=kLoop, calls=%fused_computation.51 | loop fusion | flops 264192 | bytes 792576 | tf_op jit(solution)/shard_map/mul | solution.py:47
  34.0 1.8 %collective-permute-done.3 = s32[8,1,128]{2,1,0:T(1,128)S(1)} collective-permute-done((s32[8,1,128]{2,1,0:T(1,128)S(1)}, s32[8,1,128]{2,1,0:T(1,128)S(1)}, u32[]{:S(2)}, u32[]{:S(2)}) %collective-permute-start.3) | collective-permute-done | bytes 4128 | tf_op jit(solution)/shard_map/ppermute | solution.py:10
  35.8 4.1 %collective-permute-start.1 = (f32[5,2,64,128]{3,2,1,0:T(8,128)}, f32[5,2,64,128]{3,2,1,0:T(8,128)}, u32[]{:S(2)}, u32[]{:S(2)}) collective-permute-start(f32[5,2,64,128]{3,2,1,0:T(8,128)} %get-tuple-element.26), channel_id=1, source_target_pairs={{0,8},{8,16},{16,24},{1,9},{9,17},{17,25},{2,10},{10,18},{18,26},{... | collective-permute-start | bytes 983048 | tf_op jit(solution)/shard_map/ppermute | solution.py:18
  39.9 0.6 slice_multiply_fusion.11
  40.6 1.0 %pad_maximum_fusion.18 = (f32[8,65,128]{2,1,0:T(8,128)}, f32[8,65,128]{2,1,0:T(8,128)}, f32[8,65,128]{2,1,0:T(8,128)}) fusion(f32[8,1,128]{2,1,0:T(1,128)S(1)} %get-tuple-element.47, f32[8,63,128]{2,1,0:T(8,128)S(1)} %slice.275, f32[8,1,128]{2,1,0:T(1,128)S(1)} %get-tuple-element.46), kind=kLoop, calls=%fused_computation.55 | loop fusion | flops 399360 | bytes 1064960 | tf_op jit(solution)/shard_map/concatenate | solution.py:90
  41.6 0.7 broadcast_compare_fusion.1
  42.3 1.3 %collective-permute-start.2 = (f32[5,2,64,128]{3,2,1,0:T(8,128)}, f32[5,2,64,128]{3,2,1,0:T(8,128)}, u32[]{:S(2)}, u32[]{:S(2)}) collective-permute-start(f32[5,2,64,128]{3,2,1,0:T(8,128)} %get-tuple-element.27), channel_id=1, source_target_pairs={{8,0},{16,8},{24,16},{9,1},{17,9},{25,17},{10,2},{18,10},{26,18},{... | collective-permute-start | bytes 983048 | tf_op jit(solution)/shard_map/ppermute | solution.py:21
  43.6 2.3 %copy.146 = f32[5,8,64,2]{3,2,1,0:T(8,128)} copy(f32[5,8,64,2]{2,1,3,0:T(8,128)} %collective-permute-done.8) | data formatting | bytes 40960 | tf_op jit(solution)/shard_map/ppermute | solution.py:21
  45.9 2.6 %maximum_select_fusion.1 = f32[5,8,64,2]{3,2,1,0:T(8,128)S(1)} fusion(f32[5,8,64,2]{3,2,1,0:T(8,128)} %copy.146, f32[5,8,64,1]{3,2,1,0:T(8,128)} %get-tuple-element.33, pred[]{:T(512)S(6)} %eq.29), kind=kLoop, calls=%fused_computation.47 | loop fusion | flops 10240 | bytes 51201 | tf_op jit(solution)/shard_map/jit(_where)/select_n | solution.py:65
  48.6 1.7 %pad_maximum_fusion.4 = f32[5,8,64,130]{3,2,1,0:T(8,128)} fusion(f32[5,8,64,2]{3,2,1,0:T(8,128)S(1)} %maximum_select_fusion.1, f32[1,8,64,128]{3,2,1,0:T(8,128)S(1)} %bitcast.36, f32[3,8,64,128]{3,2,1,0:T(8,128)S(1)} %copy-done, f32[1,8,64,128]{3,2,1,0:T(8,128)S(1)} %bitcast.44), kind=kLoop, calls=%fused_computation.11 | loop fusion | flops 998400 | bytes 2662400 | tf_op jit(solution)/shard_map/concatenate | solution.py:70
  50.3 1.5 %collective-permute-start = (s32[1,64,128]{2,1,0:T(8,128)}, s32[1,64,128]{2,1,0:T(8,128)}, u32[]{:S(2)}, u32[]{:S(2)}) collective-permute-start(s32[1,64,128]{2,1,0:T(8,128)} %slice_bitcast_fusion.5), channel_id=1, source_target_pairs={{8,0},{16,8},{24,16},{9,1},{17,9},{25,17},{10,2},{18,10},{26,18},{... | collective-permute-start | bytes 98312 | tf_op jit(solution)/shard_map/ppermute | solution.py:10
  51.8 2.4 %copy.144 = f32[5,8,64,2]{3,2,1,0:T(8,128)} copy(f32[5,8,64,2]{2,1,3,0:T(8,128)} %collective-permute-done.7) | data formatting | bytes 40960 | tf_op jit(solution)/shard_map/ppermute | solution.py:18
  54.2 2.1 %maximum_select_fusion = f32[5,8,64,2]{3,2,1,0:T(8,128)S(1)} fusion(f32[5,8,64,2]{3,2,1,0:T(8,128)} %copy.144, f32[5,8,64,1]{3,2,1,0:T(8,128)} %get-tuple-element.32, pred[]{:T(512)S(6)} %eq.28), kind=kLoop, calls=%fused_computation.46 | loop fusion | flops 10240 | bytes 51201 | tf_op jit(solution)/shard_map/jit(_where)/select_n | solution.py:60
  56.3 3.1 %maximum_maximum_fusion = (f32[5,8,64,130]{3,2,1,0:T(8,128)S(1)}, f32[5,8,64,130]{3,2,1,0:T(8,128)S(1)}) fusion(f32[1,8,64,128]{3,2,1,0:T(8,128)S(1)} %bitcast.37, f32[3,8,64,128]{3,2,1,0:T(8,128)S(1)} %copy-done, f32[1,8,64,128]{3,2,1,0:T(8,128)S(1)} %bitcast.45, f32[5,8,64,2]{3,2,1,0:T(8,128)S(1)} %maximum_select_fusion, ...), kind=kLoop, calls=%fused_computation.10 | loop fusion | flops 6656000 | bytes 4014080 | tf_op jit(solution)/shard_map/concatenate | solution.py:70
  59.5 1.4 %fusion.2 = f32[5,8,64,129]{3,2,1,0:T(8,128)S(1)} fusion(f32[5,8,64,130]{3,2,1,0:T(8,128)S(1)} %get-tuple-element.17, f32[5,8,64,130]{3,2,1,0:T(8,128)S(1)} %copy-done.3, f32[5,8,64,130]{3,2,1,0:T(8,128)S(1)} %get-tuple-element.16, f32[8,64,129]{2,1,0:T(8,128)S(1)} %copy-done.6, f32[8,64,129]{2,1,0:T(8,128)S(1)} %copy-done.5, ...), kind=kLoop, calls=%fused_computation.3 | loop fusion | flops 1981440 | bytes 7463424 | tf_op jit(solution)/shard_map/mul | solution.py:45
  60.9 1.4 %fusion.17 = f32[1,64,128]{2,1,0:T(8,128)S(1)} fusion(f32[3,8,64,128]{3,2,1,0:T(8,128)} %copy-done.4, s32[1,64,128]{2,1,0:T(8,128)} %collective-permute-done, f32[]{:T(128)} %bitcast.5, pred[]{:T(512)S(6)} %eq.25), kind=kLoop, calls=%fused_computation.77 | loop fusion | flops 32768 | bytes 98309 | tf_op jit(solution)/shard_map/jit(_where)/select_n | solution.py:87
  62.3 0.1 pad_maximum_fusion.17
  62.5 0.8 maximum_select_fusion.5
  63.3 0.1 pad_maximum_fusion.14
  63.5 0.8 maximum_select_fusion.4
  64.3 0.0 copy-start.13
  64.3 1.3 %maximum_maximum_fusion.2 = (f32[5,8,66,128]{3,2,1,0:T(8,128)S(1)}, f32[5,8,66,128]{3,2,1,0:T(8,128)S(1)}) fusion(f32[1,8,64,128]{3,2,1,0:T(8,128)S(1)} %bitcast.39, f32[3,8,64,128]{3,2,1,0:T(8,128)S(1)} %copy-done, f32[1,8,64,128]{3,2,1,0:T(8,128)S(1)} %bitcast.47, f32[5,8,2,128]{3,2,1,0:T(2,128)S(1)} %maximum_select_fusion.4, ...), kind=kLoop, calls=%fused_computation.36 | loop fusion | flops 6758400 | bytes 4096000 | tf_op jit(solution)/shard_map/concatenate | solution.py:70
  65.7 0.5 fusion.6
  66.2 0.0 collective-permute-done.2
  66.2 0.4 copy-done.12
  66.6 1.0 maximum_select_fusion.3
  67.6 0.0 copy-start.11
  67.6 0.1 pad_maximum_fusion.9
  67.7 0.0 collective-permute-done.1
  67.8 0.8 copy-done.11
  68.6 1.2 %maximum_maximum_fusion.1 = (f32[5,10,64,128]{3,2,1,0:T(8,128)S(1)}, f32[5,10,64,128]{3,2,1,0:T(8,128)S(1)}) fusion(f32[1,8,64,128]{3,2,1,0:T(8,128)S(1)} %bitcast.41, f32[3,8,64,128]{3,2,1,0:T(8,128)S(1)} %copy-done, f32[1,8,64,128]{3,2,1,0:T(8,128)S(1)} %bitcast.49, f32[5,2,64,128]{3,2,1,0:T(8,128)S(1)} %maximum_select_fusion.2, ...), kind=kLoop, calls=%fused_computation.17 | loop fusion | flops 8192000 | bytes 5242880 | tf_op jit(solution)/shard_map/concatenate | solution.py:70
  69.8 0.6 fusion.10
  70.4 0.8 fusion.12
  71.2 1.4 %slice_reduce_fusion.1 = (f32[]{:T(128)}, f32[]{:T(128)}, f32[8,64,128]{2,1,0:T(8,128)}, f32[8,64,128]{2,1,0:T(8,128)}) fusion(f32[5,8,64,128]{3,2,1,0:T(8,128)S(1)} %fusion.12), kind=kLoop, calls=%fused_computation.68 | loop fusion | flops 131070 | bytes 1048584 | tf_op jit(solution)/shard_map/reduce_sum | solution.py:118
  72.7 0.9 slice.302
  73.6 13.4 %all-reduce.1 = (f32[]{:T(128)}, f32[]{:T(128)}) all-reduce(f32[]{:T(128)} %get-tuple-element.9, f32[]{:T(128)} %get-tuple-element.8), channel_id=1, replica_groups=mesh['gx'=4,'gy'=4,'gz'=2] {'gx'}, use_global_device_ids=true, to_apply=%region_4.5 | all-reduce | flops 2 | bytes 16 | tf_op jit(solution)/shard_map/psum | solution.py:118
  87.0 15.9 %all-reduce = (f32[1]{0:T(128)}, f32[1]{0:T(128)}) all-reduce(f32[1]{0:T(128)} %bitcast.20, f32[1]{0:T(128)} %bitcast.19), channel_id=1, replica_groups=mesh['gx'=4,'gy'=4,'gz'=2] {'gy','gz'}, use_global_device_ids=true, to_apply=%region_5.6 | all-reduce | flops 2 | bytes 16 | tf_op jit(solution)/shard_map/psum | solution.py:117
  102.9 1.8 %maximum_multiply_fusion = f32[2]{0:T(128)} fusion(f32[1]{0:T(128)} %get-tuple-element.10, f32[1]{0:T(128)} %get-tuple-element.11), kind=kLoop, calls=%fused_computation.85 | loop fusion | flops 4 | bytes 16 | tf_op jit(solution)/shard_map/div | solution.py:120
  (44 shorter events, 0.3 us)
Async XLA Ops:
  3.5 7.8 %copy-start.7 = (s32[3,8,64,128]{3,2,1,0:T(8,128)S(1)}, s32[3,8,64,128]{3,2,1,0:T(8,128)}, u32[]{:S(2)}) copy-start(s32[3,8,64,128]{3,2,1,0:T(8,128)} %param.8) | copy-start | bytes 2359300
  6.0 44.3 %collective-permute-start.7 = (f32[5,8,64,2]{2,1,3,0:T(8,128)}, f32[5,8,64,2]{2,1,3,0:T(8,128)}, u32[]{:S(2)}, u32[]{:S(2)}) collective-permute-start(f32[5,8,64,2]{2,1,3,0:T(8,128)} %copy.143), channel_id=1, source_target_pairs={{0,1},{2,3},{4,5},{6,7},{8,9},{10,11},{12,13},{14,15},{16,17},{18,... | collective-permute-start | bytes 61448 | tf_op jit(solution)/shard_map/ppermute | solution.py:18
  10.0 32.3 %collective-permute-start.8 = (f32[5,8,64,2]{2,1,3,0:T(8,128)}, f32[5,8,64,2]{2,1,3,0:T(8,128)}, u32[]{:S(2)}, u32[]{:S(2)}) collective-permute-start(f32[5,8,64,2]{2,1,3,0:T(8,128)} %copy.145), channel_id=1, source_target_pairs={{1,0},{3,2},{5,4},{7,6},{9,8},{11,10},{13,12},{15,14},{17,16},{19,... | collective-permute-start | bytes 61448 | tf_op jit(solution)/shard_map/ppermute | solution.py:21
  12.4 17.3 %collective-permute-start.6 = (s32[8,64,1]{2,1,0:T(8,128)}, s32[8,64,1]{2,1,0:T(8,128)}, u32[]{:S(2)}, u32[]{:S(2)}) collective-permute-start(s32[8,64,1]{2,1,0:T(8,128)} %copy.142), channel_id=1, source_target_pairs={{1,0},{3,2},{5,4},{7,6},{9,8},{11,10},{13,12},{15,14},{17,16},{19,... | collective-permute-start | bytes 6152 | tf_op jit(solution)/shard_map/ppermute | solution.py:10
  14.3 49.1 %collective-permute-start.4 = (f32[5,8,2,128]{3,1,2,0:T(8,128)}, f32[5,8,2,128]{3,1,2,0:T(8,128)}, u32[]{:S(2)}, u32[]{:S(2)}) collective-permute-start(f32[5,8,2,128]{3,1,2,0:T(8,128)} %copy.137), channel_id=1, source_target_pairs={{0,2},{2,4},{4,6},{1,3},{3,5},{5,7},{8,10},{10,12},{12,14},{9,11},... | collective-permute-start | bytes 122888 | tf_op jit(solution)/shard_map/ppermute | solution.py:18
  19.8 42.6 %collective-permute-start.5 = (f32[5,8,2,128]{3,1,2,0:T(8,128)}, f32[5,8,2,128]{3,1,2,0:T(8,128)}, u32[]{:S(2)}, u32[]{:S(2)}) collective-permute-start(f32[5,8,2,128]{3,1,2,0:T(8,128)} %copy.139), channel_id=1, source_target_pairs={{2,0},{4,2},{6,4},{3,1},{5,3},{7,5},{10,8},{12,10},{14,12},{11,9},... | collective-permute-start | bytes 122888 | tf_op jit(solution)/shard_map/ppermute | solution.py:21
  23.2 4.4 %copy-start.4 = (f32[3,8,64,128]{3,2,1,0:T(8,128)}, f32[3,8,64,128]{3,2,1,0:T(8,128)S(1)}, u32[]{:S(2)}) copy-start(f32[3,8,64,128]{3,2,1,0:T(8,128)S(1)} %convert_multiply_fusion) | copy-start | bytes 2359300
  23.9 2.3 %copy-start.16 = (s32[6]{0:T(128)S(1)}, s32[6]{0:T(128)}, u32[]{:S(2)}) copy-start(s32[6]{0:T(128)} %param.9) | copy-start | bytes 76
  29.7 6.1 %collective-permute-start.3 = (s32[8,1,128]{2,1,0:T(1,128)S(1)}, s32[8,1,128]{2,1,0:T(1,128)S(1)}, u32[]{:S(2)}, u32[]{:S(2)}) collective-permute-start(s32[8,1,128]{2,1,0:T(1,128)S(1)} %slice_bitcast_fusion.6), channel_id=1, source_target_pairs={{2,0},{4,2},{6,4},{3,1},{5,3},{7,5},{10,8},{12,10},{14,12},{11,9},... | collective-permute-start | bytes 12296 | tf_op jit(solution)/shard_map/ppermute | solution.py:10
  35.8 32.0 %collective-permute-start.1 = (f32[5,2,64,128]{3,2,1,0:T(8,128)}, f32[5,2,64,128]{3,2,1,0:T(8,128)}, u32[]{:S(2)}, u32[]{:S(2)}) collective-permute-start(f32[5,2,64,128]{3,2,1,0:T(8,128)} %get-tuple-element.26), channel_id=1, source_target_pairs={{0,8},{8,16},{16,24},{1,9},{9,17},{17,25},{2,10},{10,18},{18,26},{... | collective-permute-start | bytes 983048 | tf_op jit(solution)/shard_map/ppermute | solution.py:18
  42.3 23.9 %collective-permute-start.2 = (f32[5,2,64,128]{3,2,1,0:T(8,128)}, f32[5,2,64,128]{3,2,1,0:T(8,128)}, u32[]{:S(2)}, u32[]{:S(2)}) collective-permute-start(f32[5,2,64,128]{3,2,1,0:T(8,128)} %get-tuple-element.27), channel_id=1, source_target_pairs={{8,0},{16,8},{24,16},{9,1},{17,9},{25,17},{10,2},{18,10},{26,18},{... | collective-permute-start | bytes 983048 | tf_op jit(solution)/shard_map/ppermute | solution.py:21
  45.9 2.6 %copy-start = (f32[3,8,64,128]{3,2,1,0:T(8,128)S(1)}, f32[3,8,64,128]{3,2,1,0:T(8,128)}, u32[]{:S(2)}) copy-start(f32[3,8,64,128]{3,2,1,0:T(8,128)} %param.6) | copy-start | bytes 2359300
  45.9 2.6 %copy-start.1 = (f32[8,64,128]{2,1,0:T(8,128)S(1)}, f32[8,64,128]{2,1,0:T(8,128)}, u32[]{:S(2)}) copy-start(f32[8,64,128]{2,1,0:T(8,128)} %param.7) | copy-start | bytes 786436
  45.9 2.6 %copy-start.2 = (f32[8,64,128]{2,1,0:T(8,128)S(1)}, f32[8,64,128]{2,1,0:T(8,128)}, u32[]{:S(2)}) copy-start(f32[8,64,128]{2,1,0:T(8,128)} %param.5) | copy-start | bytes 786436
  50.3 10.6 %collective-permute-start = (s32[1,64,128]{2,1,0:T(8,128)}, s32[1,64,128]{2,1,0:T(8,128)}, u32[]{:S(2)}, u32[]{:S(2)}) collective-permute-start(s32[1,64,128]{2,1,0:T(8,128)} %slice_bitcast_fusion.5), channel_id=1, source_target_pairs={{8,0},{16,8},{24,16},{9,1},{17,9},{25,17},{10,2},{18,10},{26,18},{... | collective-permute-start | bytes 98312 | tf_op jit(solution)/shard_map/ppermute | solution.py:10
  56.3 3.1 %copy-start.3 = (f32[5,8,64,130]{3,2,1,0:T(8,128)S(1)}, f32[5,8,64,130]{3,2,1,0:T(8,128)}, u32[]{:S(2)}) copy-start(f32[5,8,64,130]{3,2,1,0:T(8,128)} %pad_maximum_fusion.4) | copy-start | bytes 3993604
  56.3 3.1 %copy-start.5 = (f32[8,64,129]{2,1,0:T(8,128)S(1)}, f32[8,64,129]{2,1,0:T(8,128)}, u32[]{:S(2)}) copy-start(f32[8,64,129]{2,1,0:T(8,128)} %get-tuple-element.38) | copy-start | bytes 792580
  56.3 3.1 %copy-start.6 = (f32[8,64,129]{2,1,0:T(8,128)S(1)}, f32[8,64,129]{2,1,0:T(8,128)}, u32[]{:S(2)}) copy-start(f32[8,64,129]{2,1,0:T(8,128)} %get-tuple-element.39) | copy-start | bytes 792580
  60.9 1.6 %copy-start.15 = (f32[5,8,1,128]{3,2,1,0:T(1,128)S(1)}, f32[5,8,1,128]{3,2,1,0:T(1,128)}, u32[]{:S(2)}) copy-start(f32[5,8,1,128]{3,2,1,0:T(1,128)} %get-tuple-element.31) | copy-start | bytes 61444
  62.5 1.0 copy-start.14
  64.3 1.3 %copy-start.8 = (f32[8,65,128]{2,1,0:T(8,128)S(1)}, f32[8,65,128]{2,1,0:T(8,128)}, u32[]{:S(2)}) copy-start(f32[8,65,128]{2,1,0:T(8,128)} %get-tuple-element.43) | copy-start | bytes 798724
  64.3 1.3 %copy-start.9 = (f32[8,65,128]{2,1,0:T(8,128)S(1)}, f32[8,65,128]{2,1,0:T(8,128)}, u32[]{:S(2)}) copy-start(f32[8,65,128]{2,1,0:T(8,128)} %get-tuple-element.44) | copy-start | bytes 798724
  64.3 1.3 %copy-start.10 = (f32[8,65,128]{2,1,0:T(8,128)S(1)}, f32[8,65,128]{2,1,0:T(8,128)}, u32[]{:S(2)}) copy-start(f32[8,65,128]{2,1,0:T(8,128)} %get-tuple-element.45) | copy-start | bytes 798724
  64.3 1.3 %copy-start.13 = (pred[8,65,128]{2,1,0:T(8,128)(4,1)S(1)}, pred[8,65,128]{2,1,0:T(8,128)(4,1)}, u32[]{:S(2)}) copy-start(pred[8,65,128]{2,1,0:T(8,128)(4,1)} %broadcast_compare_fusion.1) | copy-start | bytes 199684
  65.7 0.9 copy-start.12
  67.6 0.9 copy-start.11
